TPU v7x, 256 devices: a whole 4x4x8 slice. The times are simulated.
256 devices in a mesh: row: 32 (over z, y_lo, core), col: 8 (over y_hi, x).
Axes of the slice: x: 4, y: 4 (y_hi: 2, y_lo: 2; y = y_hi * 2 + y_lo), z: 8, core: 2. Of those that a mesh axis runs over, the one named last changes fastest.
Arguments:
- embeddings: bfloat16 [4096, 512], P('row'), may hold values from -16 to 16
- centers: bfloat16 [524288, 512], P(('row', 'col')), may hold values from -50 to 50
- labels: int32 [4096], replicated, may hold values from 0 to 524287
Outputs:
- loss: float32 [4096], P('row')
All inputs are finite; a program needn't handle non-finite values.
Results may differ from a plain program's by a relative error of at most 0.00062.
Values may be sent and summed in bfloat16 or wider, within the bound.
No kernel may reach another device: no remote copies, remote signals or barrier semaphores. Data moves between devices by JAX's collectives and lax.ppermute only.
A program may use at most 64 MiB of HBM per device.

v0:
```python
import functools
import math

import jax
import jax.numpy as jnp
from jax import lax
from jax.experimental import pallas as pl
from jax.experimental.pallas import tpu as pltpu
from jax.sharding import Mesh
from jax.sharding import PartitionSpec as P


AXES = ("z", "yl", "co", "yh", "x")
ROW = ("z", "yl", "co")
SAME_CORE = ("z", "yl", "yh", "x")

f32 = jnp.float32
bf16 = jnp.bfloat16
logit_scale = 128.0
margin_angle = 0.5
SCALE2 = logit_scale * math.log2(math.e)
NEVER = -4.0
SHIFT = 80.0
UNROLL = 8


def unit_rows(values):
    values = values.astype(f32)
    length = jnp.sqrt(jnp.sum(values * values, axis=1, keepdims=True))
    return (values / jnp.maximum(length, 1.0)).astype(bf16)


def margin_cos(cosine):
    sine = jnp.sqrt(jnp.maximum(1.0 - cosine * cosine, 0.0))
    return cosine * math.cos(margin_angle) - sine * math.sin(margin_angle)


def unit_kernel(*refs):
    at = 0
    for ref in refs[:-1]:
        refs[-1][at : at + ref.shape[0], :] = unit_rows(ref[...])
        at += ref.shape[0]


def unit_call(*parts):
    rows, width = sum(p.shape[0] for p in parts), parts[0].shape[1]
    return pl.pallas_call(
        unit_kernel,
        out_shape=jax.ShapeDtypeStruct((rows, width), bf16),
        in_specs=[pl.BlockSpec(memory_space=pltpu.VMEM)] * len(parts),
        out_specs=pl.BlockSpec(memory_space=pltpu.VMEM),
        compiler_params=pltpu.CompilerParams(vmem_limit_bytes=8 * 2**20),
        cost_estimate=pl.CostEstimate(
            flops=rows * 2**19, bytes_accessed=rows * width * 4, transcendentals=rows
        ),
    )(*parts)


def centers_kernel(raw_ref, out_ref, held, sems):
    pieces = sems.shape[0]
    rows = out_ref.shape[0] // pieces
    copies = [
        pltpu.make_async_copy(
            raw_ref.at[pl.ds(i * rows, rows)], held.at[pl.ds(i * rows, rows)], sems.at[i]
        )
        for i in range(pieces)
    ]
    for copy in copies:
        copy.start()
    for i, copy in enumerate(copies):
        copy.wait()
        out_ref[i * rows : (i + 1) * rows, :] = unit_rows(held[i * rows : (i + 1) * rows, :])


def unit_centers(centers, pieces=8):
    return pl.pallas_call(
        centers_kernel,
        out_shape=jax.ShapeDtypeStruct(centers.shape, bf16),
        in_specs=[pl.BlockSpec(memory_space=pltpu.MemorySpace.HBM)],
        out_specs=pl.BlockSpec(memory_space=pltpu.VMEM),
        scratch_shapes=[pltpu.VMEM(centers.shape, bf16), pltpu.SemaphoreType.DMA((pieces,))],
        compiler_params=pltpu.CompilerParams(vmem_limit_bytes=50 * 2**20),
        cost_estimate=pl.CostEstimate(
            flops=centers.shape[0] * 2**19,
            bytes_accessed=centers.size * 4,
            transcendentals=centers.shape[0],
        ),
        name="centers",
    )(centers)


def block_of(step, flip):
    depth = lax.axis_size("z")
    z = lax.rem(lax.axis_index("z") + step % depth, depth)
    yl = lax.axis_index("yl")
    return z, (1 - yl if flip else yl)


def first_class(core, half):
    z, yl = lax.axis_index("z"), lax.axis_index("yl")
    col = lax.axis_index("yh") * lax.axis_size("x") + lax.axis_index("x")
    cols = lax.axis_size("yh") * lax.axis_size("x")
    return (((z * 2 + yl) * 2 + core) * cols + col) * half


def stats_kernel(places, chunk, lab_ref, own_ref, other_ref, *refs):
    count = len(places)
    e_refs, (out_ref, e_all, s_own, s_other) = refs[:count], refs[-4:]
    rows, half = e_all.shape[0], own_ref.shape[0]
    co = lax.axis_index("co")
    own_first, other_first = first_class(co, half), first_class(1 - co, half)
    wanted, blocks, at = [], [], 0
    for ref, steps in zip(e_refs, places):
        e_all[at : at + ref.shape[0], :] = ref[...]
        at += ref.shape[0]
        for step, flip in steps:
            z, yl = block_of(step, flip)
            line = lab_ref[pl.ds(z * 4 + yl * 2 + co, 1), :]
            own, other = line - own_first, line - other_first
            in_own = (own >= 0) & (own < half)
            in_other = (other >= 0) & (other < half)
            wanted.append(jnp.where(in_own, own, jnp.where(in_other, other + half, -100)))
            blocks.append(z * 2 + yl)
    wanted = jnp.concatenate(wanted, axis=1) if len(wanted) > 1 else wanted[0]
    place = jnp.broadcast_to(wanted, (8, rows)) - lax.broadcasted_iota(jnp.int32, (8, rows), 0)
    turns = half // chunk

    def product(index, c_ref, s_ref):
        s_ref[...] = lax.dot_general(
            c_ref[pl.ds(index * chunk, chunk), :],
            e_all[...],
            (((1,), (1,)), ((), ())),
            preferred_element_type=f32,
        )

    def finish(total, found, shift):
        found = jnp.max(found, axis=0, keepdims=True)
        here = found > NEVER
        margin = margin_cos(found)
        if shift is None:
            peak, total = total
            top = jnp.max(peak, axis=0, keepdims=True)
            top = jnp.where(here, jnp.maximum(top, margin), top)
            total, shift = total * jnp.exp2((peak - top) * SCALE2), top * SCALE2
        total = jnp.sum(total, axis=0, keepdims=True)
        both = total + jnp.where(here, jnp.exp2(margin * SCALE2 - shift), 0.0)
        log_total = (jnp.log2(both) + shift) * math.log(2.0)
        target = jnp.where(here, logit_scale * margin, 0.0)
        copies = out_ref.shape[0] // 16
        for b, block in enumerate(blocks):
            part = slice(b * 128, (b + 1) * 128)
            line = jnp.concatenate([log_total[:, part], target[:, part]], axis=1)
            spot = pl.multiple_of(block * copies, copies)
            out_ref[pl.ds(spot, copies)] = jnp.broadcast_to(line[None], (copies, 1, 256))
        return total

    def fold(first, s_ref, state):
        sums, found = list(state[:-1]), state[-1]
        here = place - first
        for j in range(chunk // 8):
            cosine = s_ref[j * 8 : (j + 1) * 8, :]
            hit = here == j * 8
            found = jnp.where(hit, cosine, found)
            term = jnp.exp2(jnp.where(hit, NEVER, cosine) * SCALE2 - SHIFT)
            sums[j % len(sums)] = sums[j % len(sums)] + term
        return (*sums, found)

    product(0, own_ref, s_own)

    def body(k, state):
        for turn in range(UNROLL):
            t = k * UNROLL + turn
            product(t, other_ref, s_other)
            state = fold(t * chunk, s_own, state)
            product(jnp.minimum(t + 1, turns - 1), own_ref, s_own)
            state = fold(half + t * chunk, s_other, state)
        return state

    zero, none = jnp.zeros((8, rows), f32), jnp.full((8, rows), 2 * NEVER, f32)
    state = lax.fori_loop(0, turns // UNROLL, body, (zero,) * (1024 // rows) + (none,))
    total = finish(functools.reduce(jnp.add, state[:-1]), state[-1], SHIFT)

    @pl.when(jnp.min(total) < 2.0**-89)
    def _():
        def careful(first, s_ref, state):
            def one(j, state):
                peak, total, found = state
                cosine = s_ref[pl.ds(pl.multiple_of(j * 8, 8), 8), :]
                hit = place == first + j * 8
                found = jnp.where(hit, cosine, found)
                cosine = jnp.where(hit, NEVER, cosine)
                top = jnp.maximum(peak, cosine)
                total = total * jnp.exp2((peak - top) * SCALE2) + jnp.exp2((cosine - top) * SCALE2)
                return top, total, found

            return lax.fori_loop(0, chunk // 8, one, state)

        def again(k, state):
            product(k, own_ref, s_own)
            state = careful(k * chunk, s_own, state)
            product(k, other_ref, s_other)
            return careful(half + k * chunk, s_other, state)

        peak, total, found = lax.fori_loop(0, turns, again, (none * 0.5, zero, none))
        finish((peak, total), found, None)


def stats_call(board, parts, places, own, other, labels):
    rows, width = sum(p.shape[0] for p in parts), own.shape[1]
    classes = own.shape[0] + other.shape[0]
    shape = (16 * lax.axis_size("yh") * lax.axis_size("x"), 1, 256)
    chunk = 256
    boards = () if board is None else (board,)
    return pl.pallas_call(
        functools.partial(stats_kernel, tuple(places), chunk),
        out_shape=jax.ShapeDtypeStruct(shape, f32),
        in_specs=[pl.BlockSpec(memory_space=pltpu.VMEM)] * (3 + len(parts))
        + [pl.BlockSpec(memory_space=pltpu.VMEM)] * len(boards),
        out_specs=pl.BlockSpec(memory_space=pltpu.VMEM),
        scratch_shapes=[
            pltpu.VMEM((rows, width), bf16),
            pltpu.VMEM((chunk, rows), f32),
            pltpu.VMEM((chunk, rows), f32),
        ],
        input_output_aliases={3 + len(parts): 0} if boards else {},
        compiler_params=pltpu.CompilerParams(vmem_limit_bytes=16 * 2**20),
        cost_estimate=pl.CostEstimate(
            flops=2 * rows * classes * width,
            bytes_accessed=classes * width * 2,
            transcendentals=rows * classes,
        ),
    )(labels, own, other, *parts, *boards)


def moved(value, axis, by):
    n = lax.axis_size(axis)
    return lax.ppermute(value, axis, [(i, (i + by) % n) for i in range(n)])


def to_lower(value):
    spots = [(yl, yh) for yl in range(2) for yh in range(2)]
    pairs = []
    for yl, yh in spots:
        y = (yh * 2 + yl + (1 if yl else -1)) % 4
        pairs.append((spots.index((yl, yh)), spots.index((y % 2, y // 2))))
    return lax.ppermute(value, ("yl", "yh"), pairs)


def crossed(value):
    depth = lax.axis_size("z")
    pairs = [(z * 2 + yl, (z - 1) % depth * 2 + 1 - yl) for z in range(depth) for yl in range(2)]
    return lax.ppermute(value, ("z", "yl"), pairs)


def shards(embeddings, centers, labels):
    fence = lax.optimization_barrier
    up1 = moved(embeddings, "z", 1)
    down1 = moved(embeddings, "z", -1)
    beside = moved(embeddings, "yl", 1)
    lines = labels.reshape(-1, 128)
    own = unit_centers(centers)
    other = moved(own, "co", 1)

    up1, down1, own = fence((up1, down1, own))
    up2 = moved(up1, "z", 1)
    down2 = moved(down1, "z", -1)
    pair1 = unit_call(up1, down1)
    side1 = moved(pair1, "yl", 1)
    mine = unit_call(embeddings, beside)
    board = stats_call(None, [mine], [[(0, 0), (0, 1)]], own, other, lines)

    up2, down2, board = fence((up2, down2, board))
    up3 = moved(up2, "z", 1)
    down3 = moved(down2, "z", -1)
    pair2 = unit_call(up2, down2)
    side2 = moved(pair2, "yl", 1)
    board = stats_call(
        board, [pair1, side1], [[(-1, 0), (1, 0)], [(-1, 1), (1, 1)]], own, other, lines
    )

    up3, down3, board = fence((up3, down3, board))
    pair3 = unit_call(up3, down3)
    side3 = to_lower(pair3)
    far, far_side = moved(up3, "z", 1), crossed(down3)
    board = stats_call(
        board, [pair2, pair3], [[(-2, 0), (2, 0)], [(-3, 0), (3, 0)]], own, other, lines
    )
    far, far_side, side2, board = fence((far, far_side, side2, board))
    opposite = unit_call(far, far_side)
    board = stats_call(
        board, [side2, opposite], [[(-2, 1), (2, 1)], [(4, 0), (4, 1)]], own, other, lines
    )
    side3, board = fence((side3, board))
    board = stats_call(board, [side3], [[(-3, 1), (3, 1)]], own, other, lines)

    got = lax.all_to_all(board, SAME_CORE, split_axis=0, concat_axis=0, tiled=True)
    got = got.reshape(-1, 2, 128)
    log_total, target = got[:, 0], got[:, 1]
    peak = jnp.max(log_total, axis=0)
    total = jnp.sum(jnp.exp(log_total - peak), axis=0)
    return peak + jnp.log(total) - jnp.sum(target, axis=0)


def solution(mesh):
    split = Mesh(mesh.devices.reshape(8, 2, 2, 2, 4), AXES)
    return jax.shard_map(
        shards,
        mesh=split,
        in_specs=(P(ROW, None), P(AXES, None), P()),
        out_specs=P(ROW),
        check_vma=False,
    )
```

profile of v0, /device:TPU:2, one launch (start us, length us, event | category | flops | bytes accessed | tf_op | source)
XLA Modules:
  0.0 70.9 jit_solution(4469093605977531386)
XLA Ops:
  0.0 2.4 %centers.1.own_ref = bf16[2048,512]{1,0:T(8,128)(2,1)S(1)} custom-call(bf16[2048,512]{1,0:T(8,128)(2,1)} %raw_ref.1), custom_call_target="tpu_custom_call" | custom-call | flops 1073741824 | bytes 4194304 | tf_op jit(solution)/shard_map/centers/pallas_call | solution.py:76
  2.5 5.9 %collective-permute-start.1 = (bf16[128,512]{1,0:T(8,128)(2,1)S(1)}, bf16[128,512]{1,0:T(8,128)(2,1)S(1)}, u32[]{:S(2)}, u32[]{:S(2)}) collective-permute-start(bf16[128,512]{1,0:T(8,128)(2,1)S(1)} %copy-done), channel_id=1, source_target_pairs={{0,224},{32,0},{64,32},{96,64},{128,96},{160,128},{192,160},{224,1... | collective-permute-start | bytes 393224 | tf_op jit(solution)/shard_map/ppermute | solution.py:237
  8.4 3.3 %collective-permute-done.1.refs_1_ = bf16[128,512]{1,0:T(8,128)(2,1)S(1)} collective-permute-done((bf16[128,512]{1,0:T(8,128)(2,1)S(1)}, bf16[128,512]{1,0:T(8,128)(2,1)S(1)}, u32[]{:S(2)}, u32[]{:S(2)}) %collective-permute-start.1) | collective-permute-done | bytes 131104 | tf_op jit(solution)/shard_map/ppermute | solution.py:237
  11.7 3.4 %collective-permute-done.refs_0_ = bf16[128,512]{1,0:T(8,128)(2,1)S(1)} collective-permute-done((bf16[128,512]{1,0:T(8,128)(2,1)S(1)}, bf16[128,512]{1,0:T(8,128)(2,1)S(1)}, u32[]{:S(2)}, u32[]{:S(2)}) %collective-permute-start) | collective-permute-done | bytes 131104 | tf_op jit(solution)/shard_map/ppermute | solution.py:237
  15.2 0.2 shard_map.39.refs_0_
  15.3 1.7 %collective-permute-start.8 = (bf16[256,512]{1,0:T(8,128)(2,1)S(1)}, bf16[256,512]{1,0:T(8,128)(2,1)S(1)}, u32[]{:S(2)}, u32[]{:S(2)}) collective-permute-start(bf16[256,512]{1,0:T(8,128)(2,1)S(1)} %shard_map.39.refs_0_), channel_id=1, source_target_pairs={{0,16},{16,0},{1,17},{17,1},{2,18},{18,2},{3,19},{19,3},{4,20},{20... | collective-permute-start | bytes 786440 | tf_op jit(solution)/shard_map/ppermute | solution.py:237
  17.0 0.4 collective-permute-start.5
  17.4 3.2 %collective-permute-start.4 = (bf16[128,512]{1,0:T(8,128)(2,1)S(1)}, bf16[128,512]{1,0:T(8,128)(2,1)S(1)}, u32[]{:S(2)}, u32[]{:S(2)}) collective-permute-start(bf16[128,512]{1,0:T(8,128)(2,1)S(1)} %collective-permute-done.1.refs_1_), channel_id=1, source_target_pairs={{0,224},{32,0},{64,32},{96,64},{128,96},{160,128},{192,160},{224,1... | collective-permute-start | bytes 393224 | tf_op jit(solution)/shard_map/ppermute | solution.py:237
  20.7 5.0 %collective-permute-done.5.refs_1_ = bf16[128,512]{1,0:T(8,128)(2,1)S(1)} collective-permute-done((bf16[128,512]{1,0:T(8,128)(2,1)S(1)}, bf16[128,512]{1,0:T(8,128)(2,1)S(1)}, u32[]{:S(2)}, u32[]{:S(2)}) %collective-permute-start.5) | collective-permute-done | bytes 131104 | tf_op jit(solution)/shard_map/ppermute | solution.py:237
  25.7 0.2 shard_map.37.refs_0_
  25.9 1.8 %shard_map.38.refs_2_ = f32[128,1,256]{2,1,0:T(1,128)S(1)} custom-call(s32[32,128]{1,0:T(8,128)S(1)} %bitcast.3, bf16[2048,512]{1,0:T(8,128)(2,1)S(1)} %centers.1.own_ref, bf16[2048,512]{1,0:T(8,128)(2,1)S(1)} %collective-permute-done.2.other_ref, bf16[256,512]{1,0:T(8,128)(2,1)S(1)} %shard_map.37.refs_0_), custom_call_target="tpu_custom_call" | custom-call | flops 1073741824 | bytes 4194304 | tf_op jit(solution)/shard_map/pallas_call | solution.py:214
  27.8 3.2 %collective-permute-start.7 = (bf16[128,512]{1,0:T(8,128)(2,1)S(1)}, bf16[128,512]{1,0:T(8,128)(2,1)S(1)}, u32[]{:S(2)}, u32[]{:S(2)}) collective-permute-start(bf16[128,512]{1,0:T(8,128)(2,1)S(1)} %collective-permute-done.4.refs_1_), channel_id=1, source_target_pairs={{0,224},{32,0},{64,32},{96,64},{128,96},{160,128},{192,160},{224,1... | collective-permute-start | bytes 393224 | tf_op jit(solution)/shard_map/ppermute | solution.py:237
  31.0 0.2 shard_map.42.refs_0_
  31.2 1.8 %collective-permute-start.12 = (bf16[256,512]{1,0:T(8,128)(2,1)S(1)}, bf16[256,512]{1,0:T(8,128)(2,1)S(1)}, u32[]{:S(2)}, u32[]{:S(2)}) collective-permute-start(bf16[256,512]{1,0:T(8,128)(2,1)S(1)} %shard_map.42.refs_0_), channel_id=1, source_target_pairs={{0,16},{16,0},{1,17},{17,1},{2,18},{18,2},{3,19},{19,3},{4,20},{20... | collective-permute-start | bytes 786440 | tf_op jit(solution)/shard_map/ppermute | solution.py:237
  33.0 2.9 %shard_map.40.refs_2_ = f32[128,1,256]{2,1,0:T(1,128)S(1)} custom-call(s32[32,128]{1,0:T(8,128)S(1)} %bitcast.4, bf16[2048,512]{1,0:T(8,128)(2,1)S(1)} %centers.1.own_ref, bf16[2048,512]{1,0:T(8,128)(2,1)S(1)} %collective-permute-done.2.other_ref, bf16[256,512]{1,0:T(8,128)(2,1)S(1)} %shard_map.39.refs_0_, ...), custom_call_target="tpu_custom_call", output_to_operand_aliasing={{}: (5, {})} | custom-call | flops 2147483648 | bytes 4194304 | tf_op jit(solution)/shard_map/pallas_call | solution.py:214
  36.0 3.1 %collective-permute-start.11 = (bf16[128,512]{1,0:T(8,128)(2,1)S(1)}, bf16[128,512]{1,0:T(8,128)(2,1)S(1)}, u32[]{:S(2)}, u32[]{:S(2)}) collective-permute-start(bf16[128,512]{1,0:T(8,128)(2,1)S(1)} %collective-permute-done.7.refs_1_), channel_id=1, source_target_pairs={{0,240},{16,224},{32,16},{48,0},{64,48},{80,32},{96,80},{112,64},{... | collective-permute-start | bytes 393224 | tf_op jit(solution)/shard_map/ppermute | solution.py:252
  39.3 3.1 %collective-permute-start.9 = (bf16[256,512]{1,0:T(8,128)(2,1)S(1)}, bf16[256,512]{1,0:T(8,128)(2,1)S(1)}, u32[]{:S(2)}, u32[]{:S(2)}) collective-permute-start(bf16[256,512]{1,0:T(8,128)(2,1)S(1)} %shard_map.41.refs_1_), channel_id=1, source_target_pairs={{0,20},{4,16},{16,4},{20,0},{1,21},{5,17},{17,5},{21,1},{2,22},{6,... | collective-permute-start | bytes 786440 | tf_op jit(solution)/shard_map/ppermute | solution.py:246
  42.4 2.9 %shard_map.43.refs_2_ = f32[128,1,256]{2,1,0:T(1,128)S(1)} custom-call(s32[32,128]{1,0:T(8,128)S(1)} %bitcast.5, bf16[2048,512]{1,0:T(8,128)(2,1)S(1)} %centers.1.own_ref, bf16[2048,512]{1,0:T(8,128)(2,1)S(1)} %collective-permute-done.2.other_ref, bf16[256,512]{1,0:T(8,128)(2,1)S(1)} %shard_map.42.refs_0_, ...), custom_call_target="tpu_custom_call", output_to_operand_aliasing={{}: (5, {})} | custom-call | flops 2147483648 | bytes 4194304 | tf_op jit(solution)/shard_map/pallas_call | solution.py:214
  45.3 0.2 shard_map.44.refs_1_
  45.4 3.1 %shard_map.45.refs_1_ = f32[128,1,256]{2,1,0:T(1,128)S(1)} custom-call(s32[32,128]{1,0:T(8,128)S(1)} %bitcast.6, bf16[2048,512]{1,0:T(8,128)(2,1)S(1)} %centers.1.own_ref, bf16[2048,512]{1,0:T(8,128)(2,1)S(1)} %collective-permute-done.2.other_ref, bf16[256,512]{1,0:T(8,128)(2,1)S(1)} %collective-permute-done.12.refs_0_, ...), custom_call_target="tpu_custom_call", output_to_operand_aliasing={{}: (5, {})} | custom-call | flops 2147483648 | bytes 4194304 | tf_op jit(solution)/shard_map/pallas_call | solution.py:214
  48.6 1.8 %shard_map.46 = f32[128,1,256]{2,1,0:T(1,128)S(1)} custom-call(s32[32,128]{1,0:T(8,128)S(1)} %bitcast.7, bf16[2048,512]{1,0:T(8,128)(2,1)S(1)} %centers.1.own_ref, bf16[2048,512]{1,0:T(8,128)(2,1)S(1)} %collective-permute-done.2.other_ref, bf16[256,512]{1,0:T(8,128)(2,1)S(1)} %collective-permute-done.9.refs_0_, ...), custom_call_target="tpu_custom_call", output_to_operand_aliasing={{}: (4, {})} | custom-call | flops 1073741824 | bytes 4194304 | tf_op jit(solution)/shard_map/pallas_call | solution.py:214
  50.3 19.9 %all_to_all.5 = f32[128,1,256]{2,1,0:T(1,128)S(1)} all-to-all(f32[128,1,256]{2,1,0:T(1,128)S(1)} %shard_map.46), channel_id=1, replica_groups=mesh['z'=8,'yl'=2,'co'=2,'yh'=2,'x'=4] {'z','yl','yh','x'}, dimensions={0} | all-to-all | bytes 262144 | tf_op jit(solution)/shard_map/all_to_all | solution.py:296
  70.2 0.2 slice_reduce_fusion.1
  70.4 0.5 add_subtract_fusion
  (21 shorter events, 0.5 us)
Async XLA Ops:
  0.0 2.5 %copy-start = (bf16[128,512]{1,0:T(8,128)(2,1)S(1)}, bf16[128,512]{1,0:T(8,128)(2,1)}, u32[]{:S(2)}) copy-start(bf16[128,512]{1,0:T(8,128)(2,1)} %refs_0_.1) | copy-start | bytes 393220
  0.0 25.9 %copy-start.1 = (s32[4096]{0:T(1024)S(1)}, s32[4096]{0:T(1024)}, u32[]{:S(2)}) copy-start(s32[4096]{0:T(1024)} %param.5) | copy-start | bytes 49156
  2.4 23.5 %collective-permute-start.2 = (bf16[2048,512]{1,0:T(8,128)(2,1)S(1)}, bf16[2048,512]{1,0:T(8,128)(2,1)S(1)}, u32[]{:S(2)}, u32[]{:S(2)}) collective-permute-start(bf16[2048,512]{1,0:T(8,128)(2,1)S(1)} %centers.1.own_ref), channel_id=1, source_target_pairs={{0,8},{8,0},{1,9},{9,1},{2,10},{10,2},{3,11},{11,3},{4,12},{12,4},... | collective-permute-start | bytes 6291464 | tf_op jit(solution)/shard_map/ppermute | solution.py:237
  2.5 9.3 %collective-permute-start.1 = (bf16[128,512]{1,0:T(8,128)(2,1)S(1)}, bf16[128,512]{1,0:T(8,128)(2,1)S(1)}, u32[]{:S(2)}, u32[]{:S(2)}) collective-permute-start(bf16[128,512]{1,0:T(8,128)(2,1)S(1)} %copy-done), channel_id=1, source_target_pairs={{0,224},{32,0},{64,32},{96,64},{128,96},{160,128},{192,160},{224,1... | collective-permute-start | bytes 393224 | tf_op jit(solution)/shard_map/ppermute | solution.py:237
  8.4 6.7 %collective-permute-start = (bf16[128,512]{1,0:T(8,128)(2,1)S(1)}, bf16[128,512]{1,0:T(8,128)(2,1)S(1)}, u32[]{:S(2)}, u32[]{:S(2)}) collective-permute-start(bf16[128,512]{1,0:T(8,128)(2,1)S(1)} %copy-done), channel_id=1, source_target_pairs={{0,32},{32,64},{64,96},{96,128},{128,160},{160,192},{192,224},{224... | collective-permute-start | bytes 393224 | tf_op jit(solution)/shard_map/ppermute | solution.py:237
  15.3 17.7 %collective-permute-start.8 = (bf16[256,512]{1,0:T(8,128)(2,1)S(1)}, bf16[256,512]{1,0:T(8,128)(2,1)S(1)}, u32[]{:S(2)}, u32[]{:S(2)}) collective-permute-start(bf16[256,512]{1,0:T(8,128)(2,1)S(1)} %shard_map.39.refs_0_), channel_id=1, source_target_pairs={{0,16},{16,0},{1,17},{17,1},{2,18},{18,2},{3,19},{19,3},{4,20},{20... | collective-permute-start | bytes 786440 | tf_op jit(solution)/shard_map/ppermute | solution.py:237
  17.0 8.7 %collective-permute-start.5 = (bf16[128,512]{1,0:T(8,128)(2,1)S(1)}, bf16[128,512]{1,0:T(8,128)(2,1)S(1)}, u32[]{:S(2)}, u32[]{:S(2)}) collective-permute-start(bf16[128,512]{1,0:T(8,128)(2,1)S(1)} %copy-done), channel_id=1, source_target_pairs={{0,16},{16,0},{1,17},{17,1},{2,18},{18,2},{3,19},{19,3},{4,20},{20... | collective-permute-start | bytes 393224 | tf_op jit(solution)/shard_map/ppermute | solution.py:237
  17.4 10.2 %collective-permute-start.3 = (bf16[128,512]{1,0:T(8,128)(2,1)S(1)}, bf16[128,512]{1,0:T(8,128)(2,1)S(1)}, u32[]{:S(2)}, u32[]{:S(2)}) collective-permute-start(bf16[128,512]{1,0:T(8,128)(2,1)S(1)} %collective-permute-done.refs_0_), channel_id=1, source_target_pairs={{0,32},{32,64},{64,96},{96,128},{128,160},{160,192},{192,224},{224... | collective-permute-start | bytes 393224 | tf_op jit(solution)/shard_map/ppermute | solution.py:237
  17.4 10.2 %collective-permute-start.4 = (bf16[128,512]{1,0:T(8,128)(2,1)S(1)}, bf16[128,512]{1,0:T(8,128)(2,1)S(1)}, u32[]{:S(2)}, u32[]{:S(2)}) collective-permute-start(bf16[128,512]{1,0:T(8,128)(2,1)S(1)} %collective-permute-done.1.refs_1_), channel_id=1, source_target_pairs={{0,224},{32,0},{64,32},{96,64},{128,96},{160,128},{192,160},{224,1... | collective-permute-start | bytes 393224 | tf_op jit(solution)/shard_map/ppermute | solution.py:237
  27.7 8.2 %collective-permute-start.6 = (bf16[128,512]{1,0:T(8,128)(2,1)S(1)}, bf16[128,512]{1,0:T(8,128)(2,1)S(1)}, u32[]{:S(2)}, u32[]{:S(2)}) collective-permute-start(bf16[128,512]{1,0:T(8,128)(2,1)S(1)} %collective-permute-done.3.refs_0_), channel_id=1, source_target_pairs={{0,32},{32,64},{64,96},{96,128},{128,160},{160,192},{192,224},{224... | collective-permute-start | bytes 393224 | tf_op jit(solution)/shard_map/ppermute | solution.py:237
  27.8 8.1 %collective-permute-start.7 = (bf16[128,512]{1,0:T(8,128)(2,1)S(1)}, bf16[128,512]{1,0:T(8,128)(2,1)S(1)}, u32[]{:S(2)}, u32[]{:S(2)}) collective-permute-start(bf16[128,512]{1,0:T(8,128)(2,1)S(1)} %collective-permute-done.4.refs_1_), channel_id=1, source_target_pairs={{0,224},{32,0},{64,32},{96,64},{128,96},{160,128},{192,160},{224,1... | collective-permute-start | bytes 393224 | tf_op jit(solution)/shard_map/ppermute | solution.py:237
  31.2 14.1 %collective-permute-start.12 = (bf16[256,512]{1,0:T(8,128)(2,1)S(1)}, bf16[256,512]{1,0:T(8,128)(2,1)S(1)}, u32[]{:S(2)}, u32[]{:S(2)}) collective-permute-start(bf16[256,512]{1,0:T(8,128)(2,1)S(1)} %shard_map.42.refs_0_), channel_id=1, source_target_pairs={{0,16},{16,0},{1,17},{17,1},{2,18},{18,2},{3,19},{19,3},{4,20},{20... | collective-permute-start | bytes 786440 | tf_op jit(solution)/shard_map/ppermute | solution.py:237
  35.9 9.4 %collective-permute-start.10 = (bf16[128,512]{1,0:T(8,128)(2,1)S(1)}, bf16[128,512]{1,0:T(8,128)(2,1)S(1)}, u32[]{:S(2)}, u32[]{:S(2)}) collective-permute-start(bf16[128,512]{1,0:T(8,128)(2,1)S(1)} %collective-permute-done.6.refs_0_), channel_id=1, source_target_pairs={{0,32},{32,64},{64,96},{96,128},{128,160},{160,192},{192,224},{224... | collective-permute-start | bytes 393224 | tf_op jit(solution)/shard_map/ppermute | solution.py:237
  36.0 9.3 %collective-permute-start.11 = (bf16[128,512]{1,0:T(8,128)(2,1)S(1)}, bf16[128,512]{1,0:T(8,128)(2,1)S(1)}, u32[]{:S(2)}, u32[]{:S(2)}) collective-permute-start(bf16[128,512]{1,0:T(8,128)(2,1)S(1)} %collective-permute-done.7.refs_1_), channel_id=1, source_target_pairs={{0,240},{16,224},{32,16},{48,0},{64,48},{80,32},{96,80},{112,64},{... | collective-permute-start | bytes 393224 | tf_op jit(solution)/shard_map/ppermute | solution.py:252
  39.3 9.3 %collective-permute-start.9 = (bf16[256,512]{1,0:T(8,128)(2,1)S(1)}, bf16[256,512]{1,0:T(8,128)(2,1)S(1)}, u32[]{:S(2)}, u32[]{:S(2)}) collective-permute-start(bf16[256,512]{1,0:T(8,128)(2,1)S(1)} %shard_map.41.refs_1_), channel_id=1, source_target_pairs={{0,20},{4,16},{16,4},{20,0},{1,21},{5,17},{17,5},{21,1},{2,22},{6,... | collective-permute-start | bytes 786440 | tf_op jit(solution)/shard_map/ppermute | solution.py:246
where the time goes:
time: 71.1 us; the launch traced here: 70.9 us
  starting transfers between devices  22.8 us (32%)
  blocking collectives  19.9 us (28%)
  Pallas kernels  15.5 us (22%)
  waiting for transfers between devices  11.8 us (17%)
  other arithmetic  0.73 us (1%)
    all_to_all x1, blocking collectives, shards(): lax.all_to_all(board, SAME_CORE, split_axis=0, concat_axis=0, tiled=True)  19.9 us
    ppermute x11, starting transfers between devices, moved(): return lax.ppermute(value, axis, [(i, (i + by) % n) for i in range(n)])  16.6 us
    pallas_call x5, Pallas kernels, stats_call(): pl.pallas_call(functools.partial(stats_kernel, tuple(places), chunk), out...  12.4 us
    ppermute x11, waiting for transfers between devices, moved(): return lax.ppermute(value, axis, [(i, (i + by) % n) for i in range(n)])  11.8 us
    ppermute x1, starting transfers between devices, crossed(): return lax.ppermute(value, ('z', 'yl'), pairs)  3.11 us
    ppermute x1, starting transfers between devices, to_lower(): return lax.ppermute(value, ('yl', 'yh'), pairs)  3.1 us
    pallas_call x1, Pallas kernels, unit_centers(): pl.pallas_call(centers_kernel, out_shape=jax.ShapeDtypeStruct(centers.sha...  2.36 us
  transfers between devices with their start and end apart: 13, of which 3 were waited for; matrix products, arithmetic and copies ran while one was open for 0% of the time, Pallas kernels for 16%

commit v1 on v0

--- a/solution.py
+++ b/solution.py
@@ -103,7 +103,7 @@
     return (((z * 2 + yl) * 2 + core) * cols + col) * half
 
 
-def stats_kernel(places, chunk, lab_ref, own_ref, other_ref, *refs):
+def stats_kernel(places, raw, chunk, lab_ref, own_ref, other_ref, *refs):
     count = len(places)
     e_refs, (out_ref, e_all, s_own, s_other) = refs[:count], refs[-4:]
     rows, half = e_all.shape[0], own_ref.shape[0]
@@ -111,7 +111,7 @@
     own_first, other_first = first_class(co, half), first_class(1 - co, half)
     wanted, blocks, at = [], [], 0
     for ref, steps in zip(e_refs, places):
-        e_all[at : at + ref.shape[0], :] = ref[...]
+        e_all[at : at + ref.shape[0], :] = unit_rows(ref[...]) if raw else ref[...]
         at += ref.shape[0]
         for step, flip in steps:
             z, yl = block_of(step, flip)
@@ -205,14 +205,14 @@
         finish((peak, total), found, None)
 
 
-def stats_call(board, parts, places, own, other, labels):
+def stats_call(board, parts, places, own, other, labels, raw=False):
     rows, width = sum(p.shape[0] for p in parts), own.shape[1]
     classes = own.shape[0] + other.shape[0]
     shape = (16 * lax.axis_size("yh") * lax.axis_size("x"), 1, 256)
     chunk = 256
     boards = () if board is None else (board,)
     return pl.pallas_call(
-        functools.partial(stats_kernel, tuple(places), chunk),
+        functools.partial(stats_kernel, tuple(places), raw, chunk),
         out_shape=jax.ShapeDtypeStruct(shape, f32),
         in_specs=[pl.BlockSpec(memory_space=pltpu.VMEM)] * (3 + len(parts))
         + [pl.BlockSpec(memory_space=pltpu.VMEM)] * len(boards),
@@ -232,6 +232,33 @@
     )(labels, own, other, *parts, *boards)
 
 
+def combine_kernel(got_ref, out_ref):
+    n = got_ref.shape[0] // 8
+    even = lax.rem(lax.broadcasted_iota(jnp.int32, (8, 128), 0), 2) == 0
+    tiles = [got_ref[i * 8 : (i + 1) * 8, :] for i in range(n)]
+    peak = functools.reduce(jnp.maximum, tiles)
+    peak = jnp.max(jnp.where(even, peak, -2.0 * logit_scale), axis=0, keepdims=True)
+    sums = [jnp.zeros((8, 128), f32)] * 4
+    for i, tile in enumerate(tiles):
+        fall = jnp.where(even, (tile - peak) * math.log2(math.e), -1000.0)
+        sums[i % 4] = sums[i % 4] + jnp.exp2(fall)
+    total = jnp.sum(functools.reduce(jnp.add, sums), axis=0, keepdims=True)
+    target = functools.reduce(jnp.add, tiles)
+    target = jnp.sum(jnp.where(even, 0.0, target), axis=0, keepdims=True)
+    out_ref[...] = peak + jnp.log(total) - target
+
+
+def combine_call(got):
+    return pl.pallas_call(
+        combine_kernel,
+        out_shape=jax.ShapeDtypeStruct((1, 128), f32),
+        in_specs=[pl.BlockSpec(memory_space=pltpu.VMEM)],
+        out_specs=pl.BlockSpec(memory_space=pltpu.VMEM),
+        compiler_params=pltpu.CompilerParams(vmem_limit_bytes=2**20),
+        name="combine",
+    )(got)
+
+
 def moved(value, axis, by):
     n = lax.axis_size(axis)
     return lax.ppermute(value, axis, [(i, (i + by) % n) for i in range(n)])
@@ -244,12 +271,6 @@
         y = (yh * 2 + yl + (1 if yl else -1)) % 4
         pairs.append((spots.index((yl, yh)), spots.index((y % 2, y // 2))))
     return lax.ppermute(value, ("yl", "yh"), pairs)
-
-
-def crossed(value):
-    depth = lax.axis_size("z")
-    pairs = [(z * 2 + yl, (z - 1) % depth * 2 + 1 - yl) for z in range(depth) for yl in range(2)]
-    return lax.ppermute(value, ("z", "yl"), pairs)
 
 
 def shards(embeddings, centers, labels):
@@ -266,8 +287,9 @@
     down2 = moved(down1, "z", -1)
     pair1 = unit_call(up1, down1)
     side1 = moved(pair1, "yl", 1)
-    mine = unit_call(embeddings, beside)
-    board = stats_call(None, [mine], [[(0, 0), (0, 1)]], own, other, lines)
+    board = stats_call(
+        None, [embeddings, beside], [[(0, 0)], [(0, 1)]], own, other, lines, raw=True
+    )
 
     up2, down2, board = fence((up2, down2, board))
     up3 = moved(up2, "z", 1)
@@ -279,26 +301,23 @@
     )
 
     up3, down3, board = fence((up3, down3, board))
+    far = moved(up3, "z", 1)
     pair3 = unit_call(up3, down3)
     side3 = to_lower(pair3)
-    far, far_side = moved(up3, "z", 1), crossed(down3)
     board = stats_call(
         board, [pair2, pair3], [[(-2, 0), (2, 0)], [(-3, 0), (3, 0)]], own, other, lines
     )
-    far, far_side, side2, board = fence((far, far_side, side2, board))
-    opposite = unit_call(far, far_side)
-    board = stats_call(
-        board, [side2, opposite], [[(-2, 1), (2, 1)], [(4, 0), (4, 1)]], own, other, lines
-    )
+    far, board = fence((far, board))
+    far_side = moved(far, "yl", 1)
+    side2, board = fence((side2, board))
+    board = stats_call(board, [side2], [[(-2, 1), (2, 1)]], own, other, lines)
     side3, board = fence((side3, board))
     board = stats_call(board, [side3], [[(-3, 1), (3, 1)]], own, other, lines)
+    far_side, board = fence((far_side, board))
+    board = stats_call(board, [far, far_side], [[(4, 0)], [(4, 1)]], own, other, lines, raw=True)
 
     got = lax.all_to_all(board, SAME_CORE, split_axis=0, concat_axis=0, tiled=True)
-    got = got.reshape(-1, 2, 128)
-    log_total, target = got[:, 0], got[:, 1]
-    peak = jnp.max(log_total, axis=0)
-    total = jnp.sum(jnp.exp(log_total - peak), axis=0)
-    return peak + jnp.log(total) - jnp.sum(target, axis=0)
+    return combine_call(got.reshape(-1, 128)).reshape(-1)
 
 
 def solution(mesh):

time: 71.1 us -> 70.4 us (level)
  blocking collectives: 19.9 us -> 22.9 us
  starting transfers between devices: 22.8 us -> 20.1 us
  waiting for transfers between devices: 11.8 us -> 10.5 us
  Pallas kernels: 15.5 us -> 16.7 us
  other arithmetic: 0.73 us -> 0 us
    ppermute x1 -> x0, starting transfers between devices: 3.11 us -> none  [crossed(): return lax.ppermute(value, ('z', 'yl'), pairs)]
    all_to_all x1, blocking collectives: 19.9 us -> 22.9 us  [shards(): lax.all_to_all(board, SAME_CORE, split_axis=0, concat_axis=0, tiled=True)]
    pallas_call x5 -> x7, Pallas kernels: 12.4 us -> 13.8 us  [the longest x6 13.2 us: stats_call(): pl.pallas_call(functools.partial(stats_kernel, tuple(places), raw, chunk)...]
    ppermute x11 -> x12, waiting for transfers between devices: 11.8 us -> 10.5 us  [moved(): return lax.ppermute(value, axis, [(i, (i + by) % n) for i in range(n)])]
    ppermute x11 -> x12, starting transfers between devices: 16.6 us -> 17.1 us  [moved(): return lax.ppermute(value, axis, [(i, (i + by) % n) for i in range(n)])]
  transfers between devices with their start and end apart: 13 -> 13, of which waited for: 3 -> 4; matrix products, arithmetic and copies ran while one was open for 0% -> 0% of each run, Pallas kernels for 16% -> 17%
where the time goes in v1:
time: 70.4 us; the launch traced here: 70.3 us
  blocking collectives  22.9 us (33%)
  starting transfers between devices  20.1 us (29%)
  Pallas kernels  16.7 us (24%)
  waiting for transfers between devices  10.5 us (15%)
    all_to_all x1, blocking collectives, shards(): lax.all_to_all(board, SAME_CORE, split_axis=0, concat_axis=0, tiled=True)  22.9 us
    ppermute x12, starting transfers between devices, moved(): return lax.ppermute(value, axis, [(i, (i + by) % n) for i in range(n)])  17.1 us
    pallas_call x6, Pallas kernels, stats_call(): pl.pallas_call(functools.partial(stats_kernel, tuple(places), raw, chunk)...  13.2 us
    ppermute x12, waiting for transfers between devices, moved(): return lax.ppermute(value, axis, [(i, (i + by) % n) for i in range(n)])  10.5 us
    ppermute x1, starting transfers between devices, to_lower(): return lax.ppermute(value, ('yl', 'yh'), pairs)  2.94 us
    pallas_call x1, Pallas kernels, unit_centers(): pl.pallas_call(centers_kernel, out_shape=jax.ShapeDtypeStruct(centers.sha...  2.36 us
  transfers between devices with their start and end apart: 13, of which 4 were waited for; matrix products, arithmetic and copies ran while one was open for 0% of the time, Pallas kernels for 17%

profile of v1, /device:TPU:2, one launch (start us, length us, event | category | flops | bytes accessed | tf_op | source)
XLA Modules:
  0.0 70.3 jit_solution(14944634284283686569)
XLA Ops:
  0.0 2.4 %centers.1.own_ref = bf16[2048,512]{1,0:T(8,128)(2,1)S(1)} custom-call(bf16[2048,512]{1,0:T(8,128)(2,1)} %raw_ref.1), custom_call_target="tpu_custom_call" | custom-call | flops 1073741824 | bytes 4194304 | tf_op jit(solution)/shard_map/centers/pallas_call | solution.py:76
  2.5 2.0 %collective-permute-start = (bf16[128,512]{1,0:T(8,128)(2,1)S(1)}, bf16[128,512]{1,0:T(8,128)(2,1)S(1)}, u32[]{:S(2)}, u32[]{:S(2)}) collective-permute-start(bf16[128,512]{1,0:T(8,128)(2,1)S(1)} %copy-done.1), channel_id=1, source_target_pairs={{0,32},{32,64},{64,96},{96,128},{128,160},{160,192},{192,224},{224... | collective-permute-start | bytes 393224 | tf_op jit(solution)/shard_map/ppermute | solution.py:264
  4.5 4.0 %collective-permute-start.1 = (bf16[128,512]{1,0:T(8,128)(2,1)S(1)}, bf16[128,512]{1,0:T(8,128)(2,1)S(1)}, u32[]{:S(2)}, u32[]{:S(2)}) collective-permute-start(bf16[128,512]{1,0:T(8,128)(2,1)S(1)} %copy-done.1), channel_id=1, source_target_pairs={{0,224},{32,0},{64,32},{96,64},{128,96},{160,128},{192,160},{224,1... | collective-permute-start | bytes 393224 | tf_op jit(solution)/shard_map/ppermute | solution.py:264
  8.5 4.0 %collective-permute-done.refs_0_ = bf16[128,512]{1,0:T(8,128)(2,1)S(1)} collective-permute-done((bf16[128,512]{1,0:T(8,128)(2,1)S(1)}, bf16[128,512]{1,0:T(8,128)(2,1)S(1)}, u32[]{:S(2)}, u32[]{:S(2)}) %collective-permute-start) | collective-permute-done | bytes 131104 | tf_op jit(solution)/shard_map/ppermute | solution.py:264
  12.5 0.2 shard_map.38.refs_0_
  12.6 1.7 %collective-permute-start.8 = (bf16[256,512]{1,0:T(8,128)(2,1)S(1)}, bf16[256,512]{1,0:T(8,128)(2,1)S(1)}, u32[]{:S(2)}, u32[]{:S(2)}) collective-permute-start(bf16[256,512]{1,0:T(8,128)(2,1)S(1)} %shard_map.38.refs_0_), channel_id=1, source_target_pairs={{0,16},{16,0},{1,17},{17,1},{2,18},{18,2},{3,19},{19,3},{4,20},{20... | collective-permute-start | bytes 786440 | tf_op jit(solution)/shard_map/ppermute | solution.py:264
  14.3 0.4 collective-permute-start.5
  14.8 3.2 %collective-permute-start.4 = (bf16[128,512]{1,0:T(8,128)(2,1)S(1)}, bf16[128,512]{1,0:T(8,128)(2,1)S(1)}, u32[]{:S(2)}, u32[]{:S(2)}) collective-permute-start(bf16[128,512]{1,0:T(8,128)(2,1)S(1)} %collective-permute-done.1.refs_1_), channel_id=1, source_target_pairs={{0,224},{32,0},{64,32},{96,64},{128,96},{160,128},{192,160},{224,1... | collective-permute-start | bytes 393224 | tf_op jit(solution)/shard_map/ppermute | solution.py:264
  18.0 5.6 %collective-permute-done.5.refs_1_ = bf16[128,512]{1,0:T(8,128)(2,1)S(1)} collective-permute-done((bf16[128,512]{1,0:T(8,128)(2,1)S(1)}, bf16[128,512]{1,0:T(8,128)(2,1)S(1)}, u32[]{:S(2)}, u32[]{:S(2)}) %collective-permute-start.5) | collective-permute-done | bytes 131104 | tf_op jit(solution)/shard_map/ppermute | solution.py:264
  23.6 1.9 %shard_map.37.refs_2_ = f32[128,1,256]{2,1,0:T(1,128)S(1)} custom-call(s32[32,128]{1,0:T(8,128)S(1)} %bitcast.4, bf16[2048,512]{1,0:T(8,128)(2,1)S(1)} %centers.1.own_ref, bf16[2048,512]{1,0:T(8,128)(2,1)S(1)} %collective-permute-done.2.other_ref, bf16[128,512]{1,0:T(8,128)(2,1)S(1)} %copy-done.1, bf16[128,512]{1,0:T(8,128)(2,1)S(1)} %collective-permute-done.5.refs_1_), custom_call_target="tpu_custom_call" | custom-call | flops 1073741824 | bytes 4194304 | tf_op jit(solution)/shard_map/pallas_call | solution.py:214
  25.6 3.2 %collective-permute-start.7 = (bf16[128,512]{1,0:T(8,128)(2,1)S(1)}, bf16[128,512]{1,0:T(8,128)(2,1)S(1)}, u32[]{:S(2)}, u32[]{:S(2)}) collective-permute-start(bf16[128,512]{1,0:T(8,128)(2,1)S(1)} %collective-permute-done.4.refs_1_), channel_id=1, source_target_pairs={{0,224},{32,0},{64,32},{96,64},{128,96},{160,128},{192,160},{224,1... | collective-permute-start | bytes 393224 | tf_op jit(solution)/shard_map/ppermute | solution.py:264
  29.0 1.8 %collective-permute-start.12 = (bf16[256,512]{1,0:T(8,128)(2,1)S(1)}, bf16[256,512]{1,0:T(8,128)(2,1)S(1)}, u32[]{:S(2)}, u32[]{:S(2)}) collective-permute-start(bf16[256,512]{1,0:T(8,128)(2,1)S(1)} %shard_map.40.refs_0_), channel_id=1, source_target_pairs={{0,16},{16,0},{1,17},{17,1},{2,18},{18,2},{3,19},{19,3},{4,20},{20... | collective-permute-start | bytes 786440 | tf_op jit(solution)/shard_map/ppermute | solution.py:264
  30.8 2.9 %shard_map.39.refs_2_ = f32[128,1,256]{2,1,0:T(1,128)S(1)} custom-call(s32[32,128]{1,0:T(8,128)S(1)} %bitcast.5, bf16[2048,512]{1,0:T(8,128)(2,1)S(1)} %centers.1.own_ref, bf16[2048,512]{1,0:T(8,128)(2,1)S(1)} %collective-permute-done.2.other_ref, bf16[256,512]{1,0:T(8,128)(2,1)S(1)} %shard_map.38.refs_0_, ...), custom_call_target="tpu_custom_call", output_to_operand_aliasing={{}: (5, {})} | custom-call | flops 2147483648 | bytes 4194304 | tf_op jit(solution)/shard_map/pallas_call | solution.py:214
  33.8 0.2 shard_map.41.refs_1_
  34.0 2.9 %collective-permute-start.11 = (bf16[256,512]{1,0:T(8,128)(2,1)S(1)}, bf16[256,512]{1,0:T(8,128)(2,1)S(1)}, u32[]{:S(2)}, u32[]{:S(2)}) collective-permute-start(bf16[256,512]{1,0:T(8,128)(2,1)S(1)} %shard_map.41.refs_1_), channel_id=1, source_target_pairs={{0,20},{4,16},{16,4},{20,0},{1,21},{5,17},{17,5},{21,1},{2,22},{6,... | collective-permute-start | bytes 786440 | tf_op jit(solution)/shard_map/ppermute | solution.py:273
  36.9 2.9 %shard_map.42.refs_1_ = f32[128,1,256]{2,1,0:T(1,128)S(1)} custom-call(s32[32,128]{1,0:T(8,128)S(1)} %bitcast.6, bf16[2048,512]{1,0:T(8,128)(2,1)S(1)} %centers.1.own_ref, bf16[2048,512]{1,0:T(8,128)(2,1)S(1)} %collective-permute-done.2.other_ref, bf16[256,512]{1,0:T(8,128)(2,1)S(1)} %shard_map.40.refs_0_, ...), custom_call_target="tpu_custom_call", output_to_operand_aliasing={{}: (5, {})} | custom-call | flops 2147483648 | bytes 4194304 | tf_op jit(solution)/shard_map/pallas_call | solution.py:214
  39.8 0.2 collective-permute-done.9.refs_0_
  40.0 0.4 collective-permute-start.10
  40.4 1.8 %shard_map.43.refs_1_ = f32[128,1,256]{2,1,0:T(1,128)S(1)} custom-call(s32[32,128]{1,0:T(8,128)S(1)} %bitcast.7, bf16[2048,512]{1,0:T(8,128)(2,1)S(1)} %centers.1.own_ref, bf16[2048,512]{1,0:T(8,128)(2,1)S(1)} %collective-permute-done.2.other_ref, bf16[256,512]{1,0:T(8,128)(2,1)S(1)} %collective-permute-done.12.refs_0_, ...), custom_call_target="tpu_custom_call", output_to_operand_aliasing={{}: (4, {})} | custom-call | flops 1073741824 | bytes 4194304 | tf_op jit(solution)/shard_map/pallas_call | solution.py:214
  42.2 2.0 %shard_map.44.refs_2_ = f32[128,1,256]{2,1,0:T(1,128)S(1)} custom-call(s32[32,128]{1,0:T(8,128)S(1)} %bitcast.8, bf16[2048,512]{1,0:T(8,128)(2,1)S(1)} %centers.1.own_ref, bf16[2048,512]{1,0:T(8,128)(2,1)S(1)} %collective-permute-done.2.other_ref, bf16[256,512]{1,0:T(8,128)(2,1)S(1)} %collective-permute-done.11.refs_0_, ...), custom_call_target="tpu_custom_call", output_to_operand_aliasing={{}: (4, {})} | custom-call | flops 1073741824 | bytes 4194304 | tf_op jit(solution)/shard_map/pallas_call | solution.py:214
  44.2 0.7 %collective-permute-done.10.refs_1_ = bf16[128,512]{1,0:T(8,128)(2,1)S(1)} collective-permute-done((bf16[128,512]{1,0:T(8,128)(2,1)S(1)}, bf16[128,512]{1,0:T(8,128)(2,1)S(1)}, u32[]{:S(2)}, u32[]{:S(2)}) %collective-permute-start.10) | collective-permute-done | bytes 131104 | tf_op jit(solution)/shard_map/ppermute | solution.py:264
  45.0 1.9 %shard_map.45 = f32[128,1,256]{2,1,0:T(1,128)S(1)} custom-call(s32[32,128]{1,0:T(8,128)S(1)} %bitcast.9, bf16[2048,512]{1,0:T(8,128)(2,1)S(1)} %centers.1.own_ref, bf16[2048,512]{1,0:T(8,128)(2,1)S(1)} %collective-permute-done.2.other_ref, bf16[128,512]{1,0:T(8,128)(2,1)S(1)} %collective-permute-done.9.refs_0_, ...), custom_call_target="tpu_custom_call", output_to_operand_aliasing={{}: (5, {})} | custom-call | flops 1073741824 | bytes 4194304 | tf_op jit(solution)/shard_map/pallas_call | solution.py:214
  46.8 22.9 %all_to_all.5 = f32[128,1,256]{2,1,0:T(1,128)S(1)} all-to-all(f32[128,1,256]{2,1,0:T(1,128)S(1)} %shard_map.45), channel_id=1, replica_groups=mesh['z'=8,'yl'=2,'co'=2,'yh'=2,'x'=4] {'z','yl','yh','x'}, dimensions={0} | all-to-all | bytes 262144 | tf_op jit(solution)/shard_map/all_to_all | solution.py:319
  69.7 0.6 combine.1
  (18 shorter events, 0.5 us)
Async XLA Ops:
  0.0 2.5 %copy-start.1 = (bf16[128,512]{1,0:T(8,128)(2,1)S(1)}, bf16[128,512]{1,0:T(8,128)(2,1)}, u32[]{:S(2)}) copy-start(bf16[128,512]{1,0:T(8,128)(2,1)} %refs_0_.1) | copy-start | bytes 393220
  0.0 23.6 %copy-start = (s32[4096]{0:T(1024)S(1)}, s32[4096]{0:T(1024)}, u32[]{:S(2)}) copy-start(s32[4096]{0:T(1024)} %param.5) | copy-start | bytes 49156
  2.4 21.2 %collective-permute-start.2 = (bf16[2048,512]{1,0:T(8,128)(2,1)S(1)}, bf16[2048,512]{1,0:T(8,128)(2,1)S(1)}, u32[]{:S(2)}, u32[]{:S(2)}) collective-permute-start(bf16[2048,512]{1,0:T(8,128)(2,1)S(1)} %centers.1.own_ref), channel_id=1, source_target_pairs={{0,8},{8,0},{1,9},{9,1},{2,10},{10,2},{3,11},{11,3},{4,12},{12,4},... | collective-permute-start | bytes 6291464 | tf_op jit(solution)/shard_map/ppermute | solution.py:264
  2.5 10.0 %collective-permute-start = (bf16[128,512]{1,0:T(8,128)(2,1)S(1)}, bf16[128,512]{1,0:T(8,128)(2,1)S(1)}, u32[]{:S(2)}, u32[]{:S(2)}) collective-permute-start(bf16[128,512]{1,0:T(8,128)(2,1)S(1)} %copy-done.1), channel_id=1, source_target_pairs={{0,32},{32,64},{64,96},{96,128},{128,160},{160,192},{192,224},{224... | collective-permute-start | bytes 393224 | tf_op jit(solution)/shard_map/ppermute | solution.py:264
  4.5 8.0 %collective-permute-start.1 = (bf16[128,512]{1,0:T(8,128)(2,1)S(1)}, bf16[128,512]{1,0:T(8,128)(2,1)S(1)}, u32[]{:S(2)}, u32[]{:S(2)}) collective-permute-start(bf16[128,512]{1,0:T(8,128)(2,1)S(1)} %copy-done.1), channel_id=1, source_target_pairs={{0,224},{32,0},{64,32},{96,64},{128,96},{160,128},{192,160},{224,1... | collective-permute-start | bytes 393224 | tf_op jit(solution)/shard_map/ppermute | solution.py:264
  12.6 18.2 %collective-permute-start.8 = (bf16[256,512]{1,0:T(8,128)(2,1)S(1)}, bf16[256,512]{1,0:T(8,128)(2,1)S(1)}, u32[]{:S(2)}, u32[]{:S(2)}) collective-permute-start(bf16[256,512]{1,0:T(8,128)(2,1)S(1)} %shard_map.38.refs_0_), channel_id=1, source_target_pairs={{0,16},{16,0},{1,17},{17,1},{2,18},{18,2},{3,19},{19,3},{4,20},{20... | collective-permute-start | bytes 786440 | tf_op jit(solution)/shard_map/ppermute | solution.py:264
  14.3 9.3 %collective-permute-start.5 = (bf16[128,512]{1,0:T(8,128)(2,1)S(1)}, bf16[128,512]{1,0:T(8,128)(2,1)S(1)}, u32[]{:S(2)}, u32[]{:S(2)}) collective-permute-start(bf16[128,512]{1,0:T(8,128)(2,1)S(1)} %copy-done.1), channel_id=1, source_target_pairs={{0,16},{16,0},{1,17},{17,1},{2,18},{18,2},{3,19},{19,3},{4,20},{20... | collective-permute-start | bytes 393224 | tf_op jit(solution)/shard_map/ppermute | solution.py:264
  14.8 10.7 %collective-permute-start.3 = (bf16[128,512]{1,0:T(8,128)(2,1)S(1)}, bf16[128,512]{1,0:T(8,128)(2,1)S(1)}, u32[]{:S(2)}, u32[]{:S(2)}) collective-permute-start(bf16[128,512]{1,0:T(8,128)(2,1)S(1)} %collective-permute-done.refs_0_), channel_id=1, source_target_pairs={{0,32},{32,64},{64,96},{96,128},{128,160},{160,192},{192,224},{224... | collective-permute-start | bytes 393224 | tf_op jit(solution)/shard_map/ppermute | solution.py:264
  14.8 10.7 %collective-permute-start.4 = (bf16[128,512]{1,0:T(8,128)(2,1)S(1)}, bf16[128,512]{1,0:T(8,128)(2,1)S(1)}, u32[]{:S(2)}, u32[]{:S(2)}) collective-permute-start(bf16[128,512]{1,0:T(8,128)(2,1)S(1)} %collective-permute-done.1.refs_1_), channel_id=1, source_target_pairs={{0,224},{32,0},{64,32},{96,64},{128,96},{160,128},{192,160},{224,1... | collective-permute-start | bytes 393224 | tf_op jit(solution)/shard_map/ppermute | solution.py:264
  25.5 8.2 %collective-permute-start.6 = (bf16[128,512]{1,0:T(8,128)(2,1)S(1)}, bf16[128,512]{1,0:T(8,128)(2,1)S(1)}, u32[]{:S(2)}, u32[]{:S(2)}) collective-permute-start(bf16[128,512]{1,0:T(8,128)(2,1)S(1)} %collective-permute-done.3.refs_0_), channel_id=1, source_target_pairs={{0,32},{32,64},{64,96},{96,128},{128,160},{160,192},{192,224},{224... | collective-permute-start | bytes 393224 | tf_op jit(solution)/shard_map/ppermute | solution.py:264
  25.6 8.1 %collective-permute-start.7 = (bf16[128,512]{1,0:T(8,128)(2,1)S(1)}, bf16[128,512]{1,0:T(8,128)(2,1)S(1)}, u32[]{:S(2)}, u32[]{:S(2)}) collective-permute-start(bf16[128,512]{1,0:T(8,128)(2,1)S(1)} %collective-permute-done.4.refs_1_), channel_id=1, source_target_pairs={{0,224},{32,0},{64,32},{96,64},{128,96},{160,128},{192,160},{224,1... | collective-permute-start | bytes 393224 | tf_op jit(solution)/shard_map/ppermute | solution.py:264
  29.0 11.0 %collective-permute-start.12 = (bf16[256,512]{1,0:T(8,128)(2,1)S(1)}, bf16[256,512]{1,0:T(8,128)(2,1)S(1)}, u32[]{:S(2)}, u32[]{:S(2)}) collective-permute-start(bf16[256,512]{1,0:T(8,128)(2,1)S(1)} %shard_map.40.refs_0_), channel_id=1, source_target_pairs={{0,16},{16,0},{1,17},{17,1},{2,18},{18,2},{3,19},{19,3},{4,20},{20... | collective-permute-start | bytes 786440 | tf_op jit(solution)/shard_map/ppermute | solution.py:264
  33.7 6.3 %collective-permute-start.9 = (bf16[128,512]{1,0:T(8,128)(2,1)S(1)}, bf16[128,512]{1,0:T(8,128)(2,1)S(1)}, u32[]{:S(2)}, u32[]{:S(2)}) collective-permute-start(bf16[128,512]{1,0:T(8,128)(2,1)S(1)} %collective-permute-done.6.refs_0_), channel_id=1, source_target_pairs={{0,32},{32,64},{64,96},{96,128},{128,160},{160,192},{192,224},{224... | collective-permute-start | bytes 393224 | tf_op jit(solution)/shard_map/ppermute | solution.py:264
  34.0 8.2 %collective-permute-start.11 = (bf16[256,512]{1,0:T(8,128)(2,1)S(1)}, bf16[256,512]{1,0:T(8,128)(2,1)S(1)}, u32[]{:S(2)}, u32[]{:S(2)}) collective-permute-start(bf16[256,512]{1,0:T(8,128)(2,1)S(1)} %shard_map.41.refs_1_), channel_id=1, source_target_pairs={{0,20},{4,16},{16,4},{20,0},{1,21},{5,17},{17,5},{21,1},{2,22},{6,... | collective-permute-start | bytes 786440 | tf_op jit(solution)/shard_map/ppermute | solution.py:273
  40.0 5.0 %collective-permute-start.10 = (bf16[128,512]{1,0:T(8,128)(2,1)S(1)}, bf16[128,512]{1,0:T(8,128)(2,1)S(1)}, u32[]{:S(2)}, u32[]{:S(2)}) collective-permute-start(bf16[128,512]{1,0:T(8,128)(2,1)S(1)} %collective-permute-done.9.refs_0_), channel_id=1, source_target_pairs={{0,16},{16,0},{1,17},{17,1},{2,18},{18,2},{3,19},{19,3},{4,20},{20... | collective-permute-start | bytes 393224 | tf_op jit(solution)/shard_map/ppermute | solution.py:264

commit v2 on v1

--- a/solution.py
+++ b/solution.py
@@ -110,8 +110,8 @@
     co = lax.axis_index("co")
     own_first, other_first = first_class(co, half), first_class(1 - co, half)
     wanted, blocks, at = [], [], 0
-    for ref, steps in zip(e_refs, places):
-        e_all[at : at + ref.shape[0], :] = unit_rows(ref[...]) if raw else ref[...]
+    for ref, steps, fresh in zip(e_refs, places, raw):
+        e_all[at : at + ref.shape[0], :] = unit_rows(ref[...]) if fresh else ref[...]
         at += ref.shape[0]
         for step, flip in steps:
             z, yl = block_of(step, flip)
@@ -205,14 +205,14 @@
         finish((peak, total), found, None)
 
 
-def stats_call(board, parts, places, own, other, labels, raw=False):
+def stats_call(board, parts, places, own, other, labels, raw=()):
     rows, width = sum(p.shape[0] for p in parts), own.shape[1]
     classes = own.shape[0] + other.shape[0]
     shape = (16 * lax.axis_size("yh") * lax.axis_size("x"), 1, 256)
     chunk = 256
     boards = () if board is None else (board,)
     return pl.pallas_call(
-        functools.partial(stats_kernel, tuple(places), raw, chunk),
+        functools.partial(stats_kernel, tuple(places), raw or (False,) * len(parts), chunk),
         out_shape=jax.ShapeDtypeStruct(shape, f32),
         in_specs=[pl.BlockSpec(memory_space=pltpu.VMEM)] * (3 + len(parts))
         + [pl.BlockSpec(memory_space=pltpu.VMEM)] * len(boards),
@@ -277,7 +277,6 @@
     fence = lax.optimization_barrier
     up1 = moved(embeddings, "z", 1)
     down1 = moved(embeddings, "z", -1)
-    beside = moved(embeddings, "yl", 1)
     lines = labels.reshape(-1, 128)
     own = unit_centers(centers)
     other = moved(own, "co", 1)
@@ -287,9 +286,9 @@
     down2 = moved(down1, "z", -1)
     pair1 = unit_call(up1, down1)
     side1 = moved(pair1, "yl", 1)
-    board = stats_call(
-        None, [embeddings, beside], [[(0, 0)], [(0, 1)]], own, other, lines, raw=True
-    )
+    late, side_seen = fence((embeddings, pair1))
+    beside = to_lower(late)
+    board = stats_call(None, [side_seen], [[(-1, 0), (1, 0)]], own, other, lines)
 
     up2, down2, board = fence((up2, down2, board))
     up3 = moved(up2, "z", 1)
@@ -297,7 +296,13 @@
     pair2 = unit_call(up2, down2)
     side2 = moved(pair2, "yl", 1)
     board = stats_call(
-        board, [pair1, side1], [[(-1, 0), (1, 0)], [(-1, 1), (1, 1)]], own, other, lines
+        board,
+        [embeddings, beside, side1],
+        [[(0, 0)], [(0, 1)], [(-1, 1), (1, 1)]],
+        own,
+        other,
+        lines,
+        raw=(True, True, False),
     )
 
     up3, down3, board = fence((up3, down3, board))
@@ -314,7 +319,7 @@
     side3, board = fence((side3, board))
     board = stats_call(board, [side3], [[(-3, 1), (3, 1)]], own, other, lines)
     far_side, board = fence((far_side, board))
-    board = stats_call(board, [far, far_side], [[(4, 0)], [(4, 1)]], own, other, lines, raw=True)
+    board = stats_call(board, [far, far_side], [[(4, 0)], [(4, 1)]], own, other, lines, raw=(True, True))
 
     got = lax.all_to_all(board, SAME_CORE, split_axis=0, concat_axis=0, tiled=True)
     return combine_call(got.reshape(-1, 128)).reshape(-1)

time: 70.4 us -> 65 us (0.923)
  waiting for transfers between devices: 10.5 us -> 4.01 us
  starting transfers between devices: 20.1 us -> 22 us
  blocking collectives: 22.9 us -> 22 us
    ppermute x12 -> x11, waiting for transfers between devices: 10.5 us -> 4.01 us  [moved(): return lax.ppermute(value, axis, [(i, (i + by) % n) for i in range(n)])]
    ppermute x1 -> x2, starting transfers between devices: 2.94 us -> 4.45 us  [to_lower(): return lax.ppermute(value, ('yl', 'yh'), pairs)]
    all_to_all x1, blocking collectives: 22.9 us -> 22 us  [shards(): lax.all_to_all(board, SAME_CORE, split_axis=0, concat_axis=0, tiled=True)]
    ppermute x12 -> x11, starting transfers between devices: 17.1 us -> 17.5 us  [moved(): return lax.ppermute(value, axis, [(i, (i + by) % n) for i in range(n)])]
  transfers between devices with their start and end apart: 13 -> 13, of which waited for: 4 -> 1; matrix products, arithmetic and copies ran while one was open for 0% -> 0% of each run, Pallas kernels for 17% -> 18%
where the time goes in v2:
time: 65 us; the launch traced here: 64.9 us
  starting transfers between devices  22 us (34%)
  blocking collectives  22 us (34%)
  Pallas kernels  16.7 us (26%)
  waiting for transfers between devices  4.01 us (6%)
    all_to_all x1, blocking collectives, shards(): lax.all_to_all(board, SAME_CORE, split_axis=0, concat_axis=0, tiled=True)  22 us
    ppermute x11, starting transfers between devices, moved(): return lax.ppermute(value, axis, [(i, (i + by) % n) for i in range(n)])  17.5 us
    pallas_call x6, Pallas kernels, stats_call(): pl.pallas_call(functools.partial(stats_kernel, tuple(places), raw or (Fal...  13.2 us
    ppermute x2, starting transfers between devices, to_lower(): return lax.ppermute(value, ('yl', 'yh'), pairs)  4.45 us
    ppermute x11, waiting for transfers between devices, moved(): return lax.ppermute(value, axis, [(i, (i + by) % n) for i in range(n)])  4.01 us
    pallas_call x1, Pallas kernels, unit_centers(): pl.pallas_call(centers_kernel, out_shape=jax.ShapeDtypeStruct(centers.sha...  2.36 us
  transfers between devices with their start and end apart: 13, of which 1 were waited for; matrix products, arithmetic and copies ran while one was open for 0% of the time, Pallas kernels for 18%

profile of v2, /device:TPU:2, one launch (start us, length us, event | category | flops | bytes accessed | tf_op | source)
XLA Modules:
  0.0 64.9 jit_solution(7244540352815160706)
XLA Ops:
  0.0 2.4 %centers.1.own_ref = bf16[2048,512]{1,0:T(8,128)(2,1)S(1)} custom-call(bf16[2048,512]{1,0:T(8,128)(2,1)} %raw_ref.1), custom_call_target="tpu_custom_call" | custom-call | flops 1073741824 | bytes 4194304 | tf_op jit(solution)/shard_map/centers/pallas_call | solution.py:76
  2.5 2.0 %collective-permute-start = (bf16[128,512]{1,0:T(8,128)(2,1)S(1)}, bf16[128,512]{1,0:T(8,128)(2,1)S(1)}, u32[]{:S(2)}, u32[]{:S(2)}) collective-permute-start(bf16[128,512]{1,0:T(8,128)(2,1)S(1)} %copy-done.1), channel_id=1, source_target_pairs={{0,32},{32,64},{64,96},{96,128},{128,160},{160,192},{192,224},{224... | collective-permute-start | bytes 393224 | tf_op jit(solution)/shard_map/ppermute | solution.py:264
  4.5 4.0 %collective-permute-start.1 = (bf16[128,512]{1,0:T(8,128)(2,1)S(1)}, bf16[128,512]{1,0:T(8,128)(2,1)S(1)}, u32[]{:S(2)}, u32[]{:S(2)}) collective-permute-start(bf16[128,512]{1,0:T(8,128)(2,1)S(1)} %copy-done.1), channel_id=1, source_target_pairs={{0,224},{32,0},{64,32},{96,64},{128,96},{160,128},{192,160},{224,1... | collective-permute-start | bytes 393224 | tf_op jit(solution)/shard_map/ppermute | solution.py:264
  8.5 4.0 %collective-permute-done.refs_0_ = bf16[128,512]{1,0:T(8,128)(2,1)S(1)} collective-permute-done((bf16[128,512]{1,0:T(8,128)(2,1)S(1)}, bf16[128,512]{1,0:T(8,128)(2,1)S(1)}, u32[]{:S(2)}, u32[]{:S(2)}) %collective-permute-start) | collective-permute-done | bytes 131104 | tf_op jit(solution)/shard_map/ppermute | solution.py:264
  12.5 0.2 shard_map.37.refs_0_
  12.6 1.7 %collective-permute-start.8 = (bf16[256,512]{1,0:T(8,128)(2,1)S(1)}, bf16[256,512]{1,0:T(8,128)(2,1)S(1)}, u32[]{:S(2)}, u32[]{:S(2)}) collective-permute-start(bf16[256,512]{1,0:T(8,128)(2,1)S(1)} %shard_map.37.refs_0_), channel_id=1, source_target_pairs={{0,16},{16,0},{1,17},{17,1},{2,18},{18,2},{3,19},{19,3},{4,20},{20... | collective-permute-start | bytes 786440 | tf_op jit(solution)/shard_map/ppermute | solution.py:264
  14.3 3.2 %collective-permute-start.4 = (bf16[128,512]{1,0:T(8,128)(2,1)S(1)}, bf16[128,512]{1,0:T(8,128)(2,1)S(1)}, u32[]{:S(2)}, u32[]{:S(2)}) collective-permute-start(bf16[128,512]{1,0:T(8,128)(2,1)S(1)} %collective-permute-done.1.refs_1_), channel_id=1, source_target_pairs={{0,224},{32,0},{64,32},{96,64},{128,96},{160,128},{192,160},{224,1... | collective-permute-start | bytes 393224 | tf_op jit(solution)/shard_map/ppermute | solution.py:264
  17.6 2.2 %collective-permute-start.7 = (bf16[128,512]{1,0:T(8,128)(2,1)S(1)}, bf16[128,512]{1,0:T(8,128)(2,1)S(1)}, u32[]{:S(2)}, u32[]{:S(2)}) collective-permute-start(bf16[128,512]{1,0:T(8,128)(2,1)S(1)} %copy-done.1), channel_id=1, source_target_pairs={{0,20},{4,16},{16,4},{20,0},{1,21},{5,17},{17,5},{21,1},{2,22},{6,... | collective-permute-start | bytes 393224 | tf_op jit(solution)/shard_map/ppermute | solution.py:273
  19.7 1.8 %shard_map.38.refs_3_ = f32[128,1,256]{2,1,0:T(1,128)S(1)} custom-call(s32[32,128]{1,0:T(8,128)S(1)} %bitcast.4, bf16[2048,512]{1,0:T(8,128)(2,1)S(1)} %centers.1.own_ref, bf16[2048,512]{1,0:T(8,128)(2,1)S(1)} %collective-permute-done.2.other_ref, bf16[256,512]{1,0:T(8,128)(2,1)S(1)} %shard_map.37.refs_0_), custom_call_target="tpu_custom_call" | custom-call | flops 1073741824 | bytes 4194304 | tf_op jit(solution)/shard_map/pallas_call | solution.py:214
  21.5 1.4 %collective-permute-start.5 = (bf16[128,512]{1,0:T(8,128)(2,1)S(1)}, bf16[128,512]{1,0:T(8,128)(2,1)S(1)}, u32[]{:S(2)}, u32[]{:S(2)}) collective-permute-start(bf16[128,512]{1,0:T(8,128)(2,1)S(1)} %collective-permute-done.3.refs_0_), channel_id=1, source_target_pairs={{0,32},{32,64},{64,96},{96,128},{128,160},{160,192},{192,224},{224... | collective-permute-start | bytes 393224 | tf_op jit(solution)/shard_map/ppermute | solution.py:264
  23.0 1.9 %collective-permute-start.6 = (bf16[128,512]{1,0:T(8,128)(2,1)S(1)}, bf16[128,512]{1,0:T(8,128)(2,1)S(1)}, u32[]{:S(2)}, u32[]{:S(2)}) collective-permute-start(bf16[128,512]{1,0:T(8,128)(2,1)S(1)} %collective-permute-done.4.refs_1_), channel_id=1, source_target_pairs={{0,224},{32,0},{64,32},{96,64},{128,96},{160,128},{192,160},{224,1... | collective-permute-start | bytes 393224 | tf_op jit(solution)/shard_map/ppermute | solution.py:264
  24.8 0.2 shard_map.40.refs_0_
  25.0 0.9 %collective-permute-start.12 = (bf16[256,512]{1,0:T(8,128)(2,1)S(1)}, bf16[256,512]{1,0:T(8,128)(2,1)S(1)}, u32[]{:S(2)}, u32[]{:S(2)}) collective-permute-start(bf16[256,512]{1,0:T(8,128)(2,1)S(1)} %shard_map.40.refs_0_), channel_id=1, source_target_pairs={{0,16},{16,0},{1,17},{17,1},{2,18},{18,2},{3,19},{19,3},{4,20},{20... | collective-permute-start | bytes 786440 | tf_op jit(solution)/shard_map/ppermute | solution.py:264
  26.0 3.0 %shard_map.39.refs_2_ = f32[128,1,256]{2,1,0:T(1,128)S(1)} custom-call(s32[32,128]{1,0:T(8,128)S(1)} %bitcast.5, bf16[2048,512]{1,0:T(8,128)(2,1)S(1)} %centers.1.own_ref, bf16[2048,512]{1,0:T(8,128)(2,1)S(1)} %collective-permute-done.2.other_ref, bf16[128,512]{1,0:T(8,128)(2,1)S(1)} %copy-done.1, ...), custom_call_target="tpu_custom_call", output_to_operand_aliasing={{}: (6, {})} | custom-call | flops 2147483648 | bytes 4194304 | tf_op jit(solution)/shard_map/pallas_call | solution.py:214
  29.0 1.0 %collective-permute-start.9 = (bf16[128,512]{1,0:T(8,128)(2,1)S(1)}, bf16[128,512]{1,0:T(8,128)(2,1)S(1)}, u32[]{:S(2)}, u32[]{:S(2)}) collective-permute-start(bf16[128,512]{1,0:T(8,128)(2,1)S(1)} %collective-permute-done.5.refs_0_), channel_id=1, source_target_pairs={{0,32},{32,64},{64,96},{96,128},{128,160},{160,192},{192,224},{224... | collective-permute-start | bytes 393224 | tf_op jit(solution)/shard_map/ppermute | solution.py:264
  29.9 0.2 shard_map.41.refs_1_
  30.1 2.3 %collective-permute-start.11 = (bf16[256,512]{1,0:T(8,128)(2,1)S(1)}, bf16[256,512]{1,0:T(8,128)(2,1)S(1)}, u32[]{:S(2)}, u32[]{:S(2)}) collective-permute-start(bf16[256,512]{1,0:T(8,128)(2,1)S(1)} %shard_map.41.refs_1_), channel_id=1, source_target_pairs={{0,20},{4,16},{16,4},{20,0},{1,21},{5,17},{17,5},{21,1},{2,22},{6,... | collective-permute-start | bytes 786440 | tf_op jit(solution)/shard_map/ppermute | solution.py:273
  32.4 2.9 %shard_map.42.refs_1_ = f32[128,1,256]{2,1,0:T(1,128)S(1)} custom-call(s32[32,128]{1,0:T(8,128)S(1)} %bitcast.6, bf16[2048,512]{1,0:T(8,128)(2,1)S(1)} %centers.1.own_ref, bf16[2048,512]{1,0:T(8,128)(2,1)S(1)} %collective-permute-done.2.other_ref, bf16[256,512]{1,0:T(8,128)(2,1)S(1)} %shard_map.40.refs_0_, ...), custom_call_target="tpu_custom_call", output_to_operand_aliasing={{}: (5, {})} | custom-call | flops 2147483648 | bytes 4194304 | tf_op jit(solution)/shard_map/pallas_call | solution.py:214
  35.3 1.3 %collective-permute-start.10 = (bf16[128,512]{1,0:T(8,128)(2,1)S(1)}, bf16[128,512]{1,0:T(8,128)(2,1)S(1)}, u32[]{:S(2)}, u32[]{:S(2)}) collective-permute-start(bf16[128,512]{1,0:T(8,128)(2,1)S(1)} %collective-permute-done.9.refs_0_), channel_id=1, source_target_pairs={{0,16},{16,0},{1,17},{17,1},{2,18},{18,2},{3,19},{19,3},{4,20},{20... | collective-permute-start | bytes 393224 | tf_op jit(solution)/shard_map/ppermute | solution.py:264
  36.6 2.0 %shard_map.43.refs_1_ = f32[128,1,256]{2,1,0:T(1,128)S(1)} custom-call(s32[32,128]{1,0:T(8,128)S(1)} %bitcast.7, bf16[2048,512]{1,0:T(8,128)(2,1)S(1)} %centers.1.own_ref, bf16[2048,512]{1,0:T(8,128)(2,1)S(1)} %collective-permute-done.2.other_ref, bf16[256,512]{1,0:T(8,128)(2,1)S(1)} %collective-permute-done.12.refs_0_, ...), custom_call_target="tpu_custom_call", output_to_operand_aliasing={{}: (4, {})} | custom-call | flops 1073741824 | bytes 4194304 | tf_op jit(solution)/shard_map/pallas_call | solution.py:214
  38.6 1.8 %shard_map.44.refs_2_ = f32[128,1,256]{2,1,0:T(1,128)S(1)} custom-call(s32[32,128]{1,0:T(8,128)S(1)} %bitcast.8, bf16[2048,512]{1,0:T(8,128)(2,1)S(1)} %centers.1.own_ref, bf16[2048,512]{1,0:T(8,128)(2,1)S(1)} %collective-permute-done.2.other_ref, bf16[256,512]{1,0:T(8,128)(2,1)S(1)} %collective-permute-done.11.refs_0_, ...), custom_call_target="tpu_custom_call", output_to_operand_aliasing={{}: (4, {})} | custom-call | flops 1073741824 | bytes 4194304 | tf_op jit(solution)/shard_map/pallas_call | solution.py:214
  40.4 1.9 %shard_map.45 = f32[128,1,256]{2,1,0:T(1,128)S(1)} custom-call(s32[32,128]{1,0:T(8,128)S(1)} %bitcast.9, bf16[2048,512]{1,0:T(8,128)(2,1)S(1)} %centers.1.own_ref, bf16[2048,512]{1,0:T(8,128)(2,1)S(1)} %collective-permute-done.2.other_ref, bf16[128,512]{1,0:T(8,128)(2,1)S(1)} %collective-permute-done.9.refs_0_, ...), custom_call_target="tpu_custom_call", output_to_operand_aliasing={{}: (5, {})} | custom-call | flops 1073741824 | bytes 4194304 | tf_op jit(solution)/shard_map/pallas_call | solution.py:214
  42.3 22.0 %all_to_all.5 = f32[128,1,256]{2,1,0:T(1,128)S(1)} all-to-all(f32[128,1,256]{2,1,0:T(1,128)S(1)} %shard_map.45), channel_id=1, replica_groups=mesh['z'=8,'yl'=2,'co'=2,'yh'=2,'x'=4] {'z','yl','yh','x'}, dimensions={0} | all-to-all | bytes 262144 | tf_op jit(solution)/shard_map/all_to_all | solution.py:324
  64.3 0.6 combine.1
  (18 shorter events, 0.1 us)
Async XLA Ops:
  0.0 2.5 %copy-start.1 = (bf16[128,512]{1,0:T(8,128)(2,1)S(1)}, bf16[128,512]{1,0:T(8,128)(2,1)}, u32[]{:S(2)}) copy-start(bf16[128,512]{1,0:T(8,128)(2,1)} %refs_0_.1) | copy-start | bytes 393220
  0.0 19.7 %copy-start = (s32[4096]{0:T(1024)S(1)}, s32[4096]{0:T(1024)}, u32[]{:S(2)}) copy-start(s32[4096]{0:T(1024)} %param.5) | copy-start | bytes 49156
  2.4 17.4 %collective-permute-start.2 = (bf16[2048,512]{1,0:T(8,128)(2,1)S(1)}, bf16[2048,512]{1,0:T(8,128)(2,1)S(1)}, u32[]{:S(2)}, u32[]{:S(2)}) collective-permute-start(bf16[2048,512]{1,0:T(8,128)(2,1)S(1)} %centers.1.own_ref), channel_id=1, source_target_pairs={{0,8},{8,0},{1,9},{9,1},{2,10},{10,2},{3,11},{11,3},{4,12},{12,4},... | collective-permute-start | bytes 6291464 | tf_op jit(solution)/shard_map/ppermute | solution.py:264
  2.5 10.0 %collective-permute-start = (bf16[128,512]{1,0:T(8,128)(2,1)S(1)}, bf16[128,512]{1,0:T(8,128)(2,1)S(1)}, u32[]{:S(2)}, u32[]{:S(2)}) collective-permute-start(bf16[128,512]{1,0:T(8,128)(2,1)S(1)} %copy-done.1), channel_id=1, source_target_pairs={{0,32},{32,64},{64,96},{96,128},{128,160},{160,192},{192,224},{224... | collective-permute-start | bytes 393224 | tf_op jit(solution)/shard_map/ppermute | solution.py:264
  4.5 8.0 %collective-permute-start.1 = (bf16[128,512]{1,0:T(8,128)(2,1)S(1)}, bf16[128,512]{1,0:T(8,128)(2,1)S(1)}, u32[]{:S(2)}, u32[]{:S(2)}) collective-permute-start(bf16[128,512]{1,0:T(8,128)(2,1)S(1)} %copy-done.1), channel_id=1, source_target_pairs={{0,224},{32,0},{64,32},{96,64},{128,96},{160,128},{192,160},{224,1... | collective-permute-start | bytes 393224 | tf_op jit(solution)/shard_map/ppermute | solution.py:264
  12.6 13.3 %collective-permute-start.8 = (bf16[256,512]{1,0:T(8,128)(2,1)S(1)}, bf16[256,512]{1,0:T(8,128)(2,1)S(1)}, u32[]{:S(2)}, u32[]{:S(2)}) collective-permute-start(bf16[256,512]{1,0:T(8,128)(2,1)S(1)} %shard_map.37.refs_0_), channel_id=1, source_target_pairs={{0,16},{16,0},{1,17},{17,1},{2,18},{18,2},{3,19},{19,3},{4,20},{20... | collective-permute-start | bytes 786440 | tf_op jit(solution)/shard_map/ppermute | solution.py:264
  14.3 7.2 %collective-permute-start.3 = (bf16[128,512]{1,0:T(8,128)(2,1)S(1)}, bf16[128,512]{1,0:T(8,128)(2,1)S(1)}, u32[]{:S(2)}, u32[]{:S(2)}) collective-permute-start(bf16[128,512]{1,0:T(8,128)(2,1)S(1)} %collective-permute-done.refs_0_), channel_id=1, source_target_pairs={{0,32},{32,64},{64,96},{96,128},{128,160},{160,192},{192,224},{224... | collective-permute-start | bytes 393224 | tf_op jit(solution)/shard_map/ppermute | solution.py:264
  14.3 7.2 %collective-permute-start.4 = (bf16[128,512]{1,0:T(8,128)(2,1)S(1)}, bf16[128,512]{1,0:T(8,128)(2,1)S(1)}, u32[]{:S(2)}, u32[]{:S(2)}) collective-permute-start(bf16[128,512]{1,0:T(8,128)(2,1)S(1)} %collective-permute-done.1.refs_1_), channel_id=1, source_target_pairs={{0,224},{32,0},{64,32},{96,64},{128,96},{160,128},{192,160},{224,1... | collective-permute-start | bytes 393224 | tf_op jit(solution)/shard_map/ppermute | solution.py:264
  17.6 8.4 %collective-permute-start.7 = (bf16[128,512]{1,0:T(8,128)(2,1)S(1)}, bf16[128,512]{1,0:T(8,128)(2,1)S(1)}, u32[]{:S(2)}, u32[]{:S(2)}) collective-permute-start(bf16[128,512]{1,0:T(8,128)(2,1)S(1)} %copy-done.1), channel_id=1, source_target_pairs={{0,20},{4,16},{16,4},{20,0},{1,21},{5,17},{17,5},{21,1},{2,22},{6,... | collective-permute-start | bytes 393224 | tf_op jit(solution)/shard_map/ppermute | solution.py:273
  21.5 7.4 %collective-permute-start.5 = (bf16[128,512]{1,0:T(8,128)(2,1)S(1)}, bf16[128,512]{1,0:T(8,128)(2,1)S(1)}, u32[]{:S(2)}, u32[]{:S(2)}) collective-permute-start(bf16[128,512]{1,0:T(8,128)(2,1)S(1)} %collective-permute-done.3.refs_0_), channel_id=1, source_target_pairs={{0,32},{32,64},{64,96},{96,128},{128,160},{160,192},{192,224},{224... | collective-permute-start | bytes 393224 | tf_op jit(solution)/shard_map/ppermute | solution.py:264
  23.0 6.0 %collective-permute-start.6 = (bf16[128,512]{1,0:T(8,128)(2,1)S(1)}, bf16[128,512]{1,0:T(8,128)(2,1)S(1)}, u32[]{:S(2)}, u32[]{:S(2)}) collective-permute-start(bf16[128,512]{1,0:T(8,128)(2,1)S(1)} %collective-permute-done.4.refs_1_), channel_id=1, source_target_pairs={{0,224},{32,0},{64,32},{96,64},{128,96},{160,128},{192,160},{224,1... | collective-permute-start | bytes 393224 | tf_op jit(solution)/shard_map/ppermute | solution.py:264
  25.0 10.3 %collective-permute-start.12 = (bf16[256,512]{1,0:T(8,128)(2,1)S(1)}, bf16[256,512]{1,0:T(8,128)(2,1)S(1)}, u32[]{:S(2)}, u32[]{:S(2)}) collective-permute-start(bf16[256,512]{1,0:T(8,128)(2,1)S(1)} %shard_map.40.refs_0_), channel_id=1, source_target_pairs={{0,16},{16,0},{1,17},{17,1},{2,18},{18,2},{3,19},{19,3},{4,20},{20... | collective-permute-start | bytes 786440 | tf_op jit(solution)/shard_map/ppermute | solution.py:264
  29.0 6.3 %collective-permute-start.9 = (bf16[128,512]{1,0:T(8,128)(2,1)S(1)}, bf16[128,512]{1,0:T(8,128)(2,1)S(1)}, u32[]{:S(2)}, u32[]{:S(2)}) collective-permute-start(bf16[128,512]{1,0:T(8,128)(2,1)S(1)} %collective-permute-done.5.refs_0_), channel_id=1, source_target_pairs={{0,32},{32,64},{64,96},{96,128},{128,160},{160,192},{192,224},{224... | collective-permute-start | bytes 393224 | tf_op jit(solution)/shard_map/ppermute | solution.py:264
  30.1 8.5 %collective-permute-start.11 = (bf16[256,512]{1,0:T(8,128)(2,1)S(1)}, bf16[256,512]{1,0:T(8,128)(2,1)S(1)}, u32[]{:S(2)}, u32[]{:S(2)}) collective-permute-start(bf16[256,512]{1,0:T(8,128)(2,1)S(1)} %shard_map.41.refs_1_), channel_id=1, source_target_pairs={{0,20},{4,16},{16,4},{20,0},{1,21},{5,17},{17,5},{21,1},{2,22},{6,... | collective-permute-start | bytes 786440 | tf_op jit(solution)/shard_map/ppermute | solution.py:273
  35.3 5.1 %collective-permute-start.10 = (bf16[128,512]{1,0:T(8,128)(2,1)S(1)}, bf16[128,512]{1,0:T(8,128)(2,1)S(1)}, u32[]{:S(2)}, u32[]{:S(2)}) collective-permute-start(bf16[128,512]{1,0:T(8,128)(2,1)S(1)} %collective-permute-done.9.refs_0_), channel_id=1, source_target_pairs={{0,16},{16,0},{1,17},{17,1},{2,18},{18,2},{3,19},{19,3},{4,20},{20... | collective-permute-start | bytes 393224 | tf_op jit(solution)/shard_map/ppermute | solution.py:264
